TPU v7x, 256 devices: a whole 4x4x8 slice. The times are simulated.
256 devices in a mesh: space: 4 (over z_hi, core), fsdp: 64 (over y, x, z_lo).
Axes of the slice: x: 4, y: 4, z: 8 (z_hi: 2, z_lo: 4; z = z_hi * 4 + z_lo), core: 2. Of those that a mesh axis runs over, the one named last changes fastest.
Arguments:
- acts: bfloat16 [64, 8, 16, 16, 512], P('fsdp', 'space'), may hold values from -16 to 16
- kernel: bfloat16 [512, 27, 256], P('fsdp'), may hold values from -0.0546875 to 0.0546875
- cotangent: bfloat16 [64, 8, 16, 16, 256], P('fsdp', 'space'), may hold values from -6 to 6
Outputs:
- outputs: bfloat16 [64, 8, 16, 16, 256], P('fsdp', 'space')
- grad_input: bfloat16 [64, 8, 16, 16, 512], P('fsdp', 'space')
- grad_kernel: float32 [512, 27, 256], P('fsdp')
All inputs are finite; a program needn't handle non-finite values.
Results may differ from a plain program's by a relative error of at most 0.0095.
Values may be sent and summed in bfloat16 or wider, within the bound.
A program may use at most 128 MiB of HBM per device.

v0:
```python
import jax
import jax.numpy as jnp
from jax import lax
from jax.sharding import PartitionSpec as P

kernel_offsets = [(i // 9 - 1, i // 3 % 3 - 1, i % 3 - 1) for i in range(27)]


def padded(block, sides, width):
    for axis, dim in sides:
        count = lax.axis_size(axis)
        forward = [(i, i + 1) for i in range(count - 1)]
        backward = [(target, source) for source, target in forward]
        low = lax.ppermute(
            lax.slice_in_dim(block, block.shape[dim] - width, None, axis=dim), axis, forward
        )
        high = lax.ppermute(lax.slice_in_dim(block, 0, width, axis=dim), axis, backward)
        block = jnp.concatenate([low, block, high], axis=dim)
    return block


def from_everyone(x, axis):
    copies = jnp.broadcast_to(x, (lax.axis_size(axis), *x.shape))
    return lax.all_to_all(copies, axis, split_axis=0, concat_axis=0, tiled=True)


def of_everyone(x, axis):
    everything = from_everyone(x, axis)
    return jnp.sum(everything.astype(jnp.float32), axis=0)


def body(acts, kernel, cotangent):
    local_acts = acts[0]
    local_grad = cotangent[0]
    slab_len = local_acts.shape[0]
    side_len = local_acts.shape[1]
    chan_in = local_acts.shape[3]
    chan_out = local_grad.shape[3]
    tap_count = len(kernel_offsets)
    padded_side = side_len + 2
    plane = padded_side * padded_side
    margin = padded_side + 1
    grid_rows = slab_len * plane
    centre = margin + plane
    acts_float = local_acts.astype(jnp.float32)
    squash = jax.nn.sigmoid(acts_float)
    hidden = (acts_float * squash).astype(jnp.bfloat16)
    joined = jnp.concatenate([hidden, local_grad], axis=3)[None]
    framed = padded(joined, (("space", 1),), 1)[0]
    framed = jnp.pad(framed, ((0, 0), (1, 1), (1, 1), (0, 0)))
    flat_all = framed.reshape((slab_len + 2) * plane, chan_in + chan_out)
    flat_all = jnp.pad(flat_all, ((margin, margin), (0, 0)))
    hidden_flat = flat_all[:, :chan_in]
    grad_flat_pad = flat_all[:, chan_in:]
    grad_centre = grad_flat_pad[centre : centre + grid_rows]

    def offset_of(tap_index):
        shift_d, shift_h, shift_w = kernel_offsets[tap_index]
        return shift_d * plane + shift_h * padded_side + shift_w

    empty_out = jnp.zeros((grid_rows, chan_out), jnp.float32)
    running = empty_out
    shard_rows = lax.all_gather(kernel, "fsdp", axis=0, tiled=True)
    channel_part = hidden_flat
    for tap_index in range(tap_count):
        begin = centre + offset_of(tap_index)
        running = running + jnp.dot(
            channel_part[begin : begin + grid_rows],
            shard_rows[:, tap_index, :],
            preferred_element_type=jnp.float32,
        )
    shard_rows = lax.all_gather(kernel, "fsdp", axis=0, tiled=True)
    row_count = shard_rows.shape[0]
    total = jnp.zeros((grid_rows, row_count), jnp.float32)
    for tap_index in range(tap_count):
        begin = centre - offset_of(tap_index)
        total = total + lax.dot_general(
            grad_flat_pad[begin : begin + grid_rows],
            shard_rows[:, tap_index, :],
            (((1,), (1,)), ((), ())),
            preferred_element_type=jnp.float32,
        )
    back = total.reshape(1, slab_len, padded_side, padded_side, row_count)
    back_inner = back[0][:, 1:-1, 1:-1, :]
    grad_input = (back_inner * squash * (1.0 + acts_float * (1.0 - squash))).astype(jnp.bfloat16)[
        None
    ]
    batch_scale = 1.0 / lax.axis_size("fsdp")
    channel_part = hidden_flat
    pieces = []
    for tap_index in range(tap_count):
        begin = centre + offset_of(tap_index)
        pieces.append(
            lax.dot_general(
                channel_part[begin : begin + grid_rows],
                grad_centre,
                (((0,), (0,)), ((), ())),
                preferred_element_type=jnp.float32,
            )
        )
    term = jnp.concatenate(pieces, axis=1)
    owned_share = lax.psum_scatter(
        term.reshape(kernel.shape[0] * lax.axis_size("fsdp"), tap_count, chan_out) * batch_scale,
        "fsdp",
        scatter_dimension=0,
        tiled=True,
    )
    grad_kernel = of_everyone(owned_share.astype(jnp.bfloat16), "space").astype(jnp.float32)
    shaped = running.reshape(slab_len, padded_side, padded_side, running.shape[-1])
    outputs = shaped[:, 1:-1, 1:-1, :].astype(jnp.bfloat16)[None]
    return (outputs, grad_input, grad_kernel)


def solution(mesh):
    return jax.shard_map(
        body,
        mesh=mesh,
        in_specs=(
            P("fsdp", "space", None, None, None),
            P("fsdp", None, None),
            P("fsdp", "space", None, None, None),
        ),
        out_specs=(
            P("fsdp", "space", None, None, None),
            P("fsdp", "space", None, None, None),
            P("fsdp", None, None),
        ),
        check_vma=False,
    )
```

profile of v0, /device:TPU:1, one launch (start us, length us, event | category | flops | bytes accessed | tf_op | source)
XLA Modules:
  0.0 806.9 jit_solution(10638212462257670923)
XLA Ops:
  7.9 1.4 fusion.4
  10.4 10.2 %collective-permute-start = (bf16[1,1,16,16,768]{4,3,2,1,0:T(8,128)(2,1)S(1)}, bf16[1,1,16,16,768]{4,3,2,1,0:T(8,128)(2,1)S(1)}, u32[]{:S(2)}, u32[]{:S(2)}) collective-permute-start(bf16[1,1,16,16,768]{4,3,2,1,0:T(8,128)(2,1)S(1)} %get-tuple-element.3), channel_id=1, source_target_pairs={{0,64},{64,128},{128,192},{1,65},{65,129},{129,193},{2,66},{66,130... | collective-permute-start | bytes 1179656 | tf_op jit(solution)/shard_map/ppermute | solution.py:14
  20.6 1.9 collective-permute-start.1
  22.5 3.6 collective-permute-done
  26.1 13.8 %collective-permute-done.1 = bf16[1,1,16,16,768]{4,3,2,1,0:T(8,128)(2,1)S(1)} collective-permute-done((bf16[1,1,16,16,768]{4,3,2,1,0:T(8,128)(2,1)S(1)}, bf16[1,1,16,16,768]{4,3,2,1,0:T(8,128)(2,1)S(1)}, u32[]{:S(2)}, u32[]{:S(2)}) %collective-permute-start.1) | collective-permute-done | bytes 393248 | tf_op jit(solution)/shard_map/ppermute | solution.py:17
  40.0 2.6 pad.8
  42.7 2.9 reshape.18
  51.8 1.3 convolution_dynamic-update-slice_fusion.21
  58.1 1.3 convolution_dynamic-update-slice_fusion.16
  60.6 1.3 convolution_dynamic-update-slice_fusion.14
  61.8 1.3 convolution_dynamic-update-slice_fusion.13
  64.3 1.3 convolution_dynamic-update-slice_fusion.11
  65.6 1.3 convolution_dynamic-update-slice_fusion.10
  66.9 1.3 convolution_dynamic-update-slice_fusion.9
  70.7 1.3 convolution_dynamic-update-slice_fusion.6
  74.4 1.3 convolution_dynamic-update-slice_fusion.3
  75.7 1.3 convolution_dynamic-update-slice_fusion.2
  76.9 1.3 convolution_dynamic-update-slice_fusion.1
  79.4 12.1 %broadcast_multiply_fusion = f32[512,6912]{0,1:T(8,128)} fusion(f32[512,6912]{0,1:T(8,128)} %convolution_dynamic-update-slice_fusion), kind=kLoop, calls=%fused_computation | loop fusion | flops 3538944 | bytes 28311552 | tf_op jit(solution)/shard_map/mul | solution.py:103
  91.5 19.9 %copy.10 = f32[512,27,256]{2,1,0:T(8,128)} copy(f32[512,27,256]{0,2,1:T(8,128)} %bitcast.124) | data formatting | bytes 28311552 | tf_op jit(solution)/shard_map/mul | solution.py:103
  111.5 195.9 %all-gather.2.cloned.1.call-done = bf16[512,27,256]{2,0,1:T(8,128)(2,1)} async-done(((bf16[8,27,256]{2,0,1:T(8,128)(2,1)}), bf16[512,27,256]{2,0,1:T(8,128)(2,1)}) %all-gather.2.cloned.1.call-update) | async-done | bytes 7077904 | tf_op jit(solution)/shard_map/all_gather | solution.py:63
  307.4 1.3 fusion.61
  308.7 1.5 fusion.89
  310.2 1.7 convolution_add_fusion.51
  331.7 401.0 %reduce-scatter.2.cloned.1.call-done = f32[8,27,256]{2,1,0:T(8,128)} async-done(((f32[512,27,256]{2,1,0:T(8,128)}), f32[8,27,256]{2,1,0:T(8,128)}) %reduce-scatter.2.cloned.1.call-update) | async-done | bytes 221200 | tf_op jit(solution)/shard_map/reduce_scatter | solution.py:102
  734.5 52.8 %all-to-all-start = ((bf16[4,8,27,256]{3,1,2,0:T(8,128)(2,1)}), bf16[4,8,27,256]{3,1,2,0:T(8,128)(2,1)}, u32[]{:S(2)}, u32[]{:S(2)}) async-start(bf16[4,8,27,256]{3,1,2,0:T(8,128)(2,1)} %broadcast_in_dim.15), calls=%async_computation.1 | async-start | bytes 884736 | tf_op jit(solution)/shard_map/all_to_all | solution.py:24
  787.3 2.2 fusion
  789.6 1.8 reshape.19
  791.6 1.8 slice_bitcast_fusion
  793.4 2.3 fusion.63
  795.7 2.6 all-to-all-done
  798.3 1.8 convert_reduce_fusion
  (78 shorter events, 43.3 us)
Async XLA Ops:
  7.2 300.3 %all-gather.2.cloned.1.call-start = ((), (), s32[]{:S(2)}) async-start(), calls=%async_computation.2 | async-start | bytes 7188480 | tf_op jit(solution)/shard_map/all_gather | solution.py:63
  7.9 724.8 %reduce-scatter.2.cloned.1.call-start = ((), (), s32[]{:S(2)}) async-start(), calls=%async_computation.3 | async-start | bytes 17039360 | tf_op jit(solution)/shard_map/reduce_scatter | solution.py:102
  10.4 15.7 %collective-permute-start = (bf16[1,1,16,16,768]{4,3,2,1,0:T(8,128)(2,1)S(1)}, bf16[1,1,16,16,768]{4,3,2,1,0:T(8,128)(2,1)S(1)}, u32[]{:S(2)}, u32[]{:S(2)}) collective-permute-start(bf16[1,1,16,16,768]{4,3,2,1,0:T(8,128)(2,1)S(1)} %get-tuple-element.3), channel_id=1, source_target_pairs={{0,64},{64,128},{128,192},{1,65},{65,129},{129,193},{2,66},{66,130... | collective-permute-start | bytes 1179656 | tf_op jit(solution)/shard_map/ppermute | solution.py:14
  20.6 19.3 %collective-permute-start.1 = (bf16[1,1,16,16,768]{4,3,2,1,0:T(8,128)(2,1)S(1)}, bf16[1,1,16,16,768]{4,3,2,1,0:T(8,128)(2,1)S(1)}, u32[]{:S(2)}, u32[]{:S(2)}) collective-permute-start(bf16[1,1,16,16,768]{4,3,2,1,0:T(8,128)(2,1)S(1)} %get-tuple-element.4), channel_id=1, source_target_pairs={{64,0},{128,64},{192,128},{65,1},{129,65},{193,129},{66,2},{130,66... | collective-permute-start | bytes 1179656 | tf_op jit(solution)/shard_map/ppermute | solution.py:17
  308.7 3.2 copy-start
  734.5 63.8 %all-to-all-start = ((bf16[4,8,27,256]{3,1,2,0:T(8,128)(2,1)}), bf16[4,8,27,256]{3,1,2,0:T(8,128)(2,1)}, u32[]{:S(2)}, u32[]{:S(2)}) async-start(bf16[4,8,27,256]{3,1,2,0:T(8,128)(2,1)} %broadcast_in_dim.15), calls=%async_computation.1 | async-start | bytes 884736 | tf_op jit(solution)/shard_map/all_to_all | solution.py:24
Sparse Core Ops, SparseCore 0:
  9.7 297.7 all-gather.1
  310.0 422.6 reduce-scatter.1
where the time goes:
time: 808 us; the launch traced here: 807 us
  waiting for transfers between devices  618 us (76%)
  starting transfers between devices  65 us (8%)
  matrix products  59.8 us (7%)
  local copies, waits for them, and re-layouts  31.2 us (4%)
  other arithmetic  18.7 us (2%)
  between operations  14.5 us (2%)
    reduce_scatter x1, waiting for transfers between devices, body(): lax.psum_scatter(term.reshape(kernel.shape[0] * lax.axis_size('fsdp'), ta...  401 us
    all_gather x1, waiting for transfers between devices, body(): shard_rows = lax.all_gather(kernel, 'fsdp', axis=0, tiled=True)  196 us
    all_to_all x1, starting transfers between devices, from_everyone(): return lax.all_to_all(copies, axis, split_axis=0, concat_axis=0, tiled=True)  52.8 us
    dot_general x27, matrix products, body(): lax.dot_general(channel_part[begin:begin + grid_rows], grad_centre, (((0,...  33.8 us
    mul x1, local copies, waits for them, and re-layouts, body(): term.reshape(kernel.shape[0] * lax.axis_size('fsdp'), tap_count, chan_out)  19.9 us
  transfers between devices with their start and end apart: 5, of which 5 were waited for; matrix products, arithmetic and copies ran while one was open for 13% of the time, Pallas kernels for 0%

commit v1 on v0

--- a/solution.py
+++ b/solution.py
@@ -60,7 +60,8 @@
 
     empty_out = jnp.zeros((grid_rows, chan_out), jnp.float32)
     running = empty_out
-    shard_rows = lax.all_gather(kernel, "fsdp", axis=0, tiled=True)
+    repeated = jnp.stack([kernel] * lax.axis_size("fsdp"))
+    shard_rows = jnp.concatenate(lax.all_to_all(repeated, "fsdp", 0, 0), axis=0)
     channel_part = hidden_flat
     for tap_index in range(tap_count):
         begin = centre + offset_of(tap_index)

time: 808 us -> 882 us (1.092)
  waiting for transfers between devices: 618 us -> 666 us
  other arithmetic: 18.7 us -> 28.1 us
    all_to_all x0 -> x1, waiting for transfers between devices: none -> 150 us  [body(): shard_rows = jnp.concatenate(lax.all_to_all(repeated, 'fsdp', 0, 0), axis=0)]
    all_gather x1, waiting for transfers between devices: 196 us -> 96.4 us  [body(): shard_rows = lax.all_gather(kernel, 'fsdp', axis=0, tiled=True)]
    mul x1, other arithmetic: 12.1 us -> 21.4 us  [body(): term.reshape(kernel.shape[0] * lax.axis_size('fsdp'), tap_count, chan_out)]
    all_to_all x0 -> x1, starting transfers between devices: none -> 9.26 us  [body(): shard_rows = jnp.concatenate(lax.all_to_all(repeated, 'fsdp', 0, 0), axis=0)]
  transfers between devices with their start and end apart: 5 -> 6, of which waited for: 5 -> 5; matrix products, arithmetic and copies ran while one was open for 13% -> 14% of each run, Pallas kernels for 0% -> 0%
where the time goes in v1:
time: 882 us; the launch traced here: 877 us
  waiting for transfers between devices  666 us (76%)
  starting transfers between devices  72.8 us (8%)
  matrix products  59 us (7%)
  local copies, waits for them, and re-layouts  36.9 us (4%)
  other arithmetic  28.1 us (3%)
  between operations  14.8 us (2%)
    reduce_scatter x1, waiting for transfers between devices, body(): lax.psum_scatter(term.reshape(kernel.shape[0] * lax.axis_size('fsdp'), ta...  406 us
    all_to_all x1, waiting for transfers between devices, body(): shard_rows = jnp.concatenate(lax.all_to_all(repeated, 'fsdp', 0, 0), axis=0)  150 us
    all_gather x1, waiting for transfers between devices, body(): shard_rows = lax.all_gather(kernel, 'fsdp', axis=0, tiled=True)  96.4 us
    all_to_all x1, starting transfers between devices, from_everyone(): return lax.all_to_all(copies, axis, split_axis=0, concat_axis=0, tiled=True)  51.3 us
    dot_general x27, matrix products, body(): lax.dot_general(channel_part[begin:begin + grid_rows], grad_centre, (((0,...  34 us
    mul x1, other arithmetic, body(): term.reshape(kernel.shape[0] * lax.axis_size('fsdp'), tap_count, chan_out)  21.4 us
    mul x1, local copies, waits for them, and re-layouts, body(): term.reshape(kernel.shape[0] * lax.axis_size('fsdp'), tap_count, chan_out)  19.9 us
  transfers between devices with their start and end apart: 6, of which 5 were waited for; matrix products, arithmetic and copies ran while one was open for 14% of the time, Pallas kernels for 0%

profile of v1, /device:TPU:1, one launch (start us, length us, event | category | flops | bytes accessed | tf_op | source)
XLA Modules:
  0.0 877.2 jit_solution(11566188731762582819)
XLA Ops:
  7.9 1.4 fusion.4
  10.4 10.2 %collective-permute-start = (bf16[1,1,16,16,768]{4,3,2,1,0:T(8,128)(2,1)S(1)}, bf16[1,1,16,16,768]{4,3,2,1,0:T(8,128)(2,1)S(1)}, u32[]{:S(2)}, u32[]{:S(2)}) collective-permute-start(bf16[1,1,16,16,768]{4,3,2,1,0:T(8,128)(2,1)S(1)} %get-tuple-element.3), channel_id=1, source_target_pairs={{0,64},{64,128},{128,192},{1,65},{65,129},{129,193},{2,66},{66,130... | collective-permute-start | bytes 1179656 | tf_op jit(solution)/shard_map/ppermute | solution.py:14
  20.6 1.9 collective-permute-start.1
  22.5 3.4 stack.2
  25.9 9.3 %all-to-all-start = ((bf16[64,8,27,256]{3,1,2,0:T(8,128)(2,1)}), bf16[64,8,27,256]{3,1,2,0:T(8,128)(2,1)}, u32[]{:S(2)}, u32[]{:S(2)}) async-start(bf16[64,8,27,256]{3,1,2,0:T(8,128)(2,1)} %stack.2), calls=%async_computation | async-start | bytes 14155776 | tf_op jit(solution)/shard_map/all_to_all | solution.py:64
  35.2 7.4 collective-permute-done.1
  42.8 2.6 pad.8
  45.5 3.1 reshape.23
  51.1 1.3 convolution_dynamic-update-slice_fusion.24
  61.1 1.3 convolution_dynamic-update-slice_fusion.16
  63.6 1.3 convolution_dynamic-update-slice_fusion.14
  67.4 1.3 convolution_dynamic-update-slice_fusion.11
  68.7 1.3 convolution_dynamic-update-slice_fusion.10
  70.0 1.3 convolution_dynamic-update-slice_fusion.9
  73.8 1.3 convolution_dynamic-update-slice_fusion.6
  77.5 1.3 convolution_dynamic-update-slice_fusion.3
  78.8 1.3 convolution_dynamic-update-slice_fusion.2
  80.0 1.3 convolution_dynamic-update-slice_fusion.1
  81.3 1.3 convolution_dynamic-update-slice_fusion
  82.6 21.4 %broadcast_multiply_fusion = f32[512,6912]{0,1:T(8,128)} fusion(f32[512,6912]{0,1:T(8,128)} %convolution_dynamic-update-slice_fusion), kind=kLoop, calls=%fused_computation.1 | loop fusion | flops 3538944 | bytes 28311552 | tf_op jit(solution)/shard_map/mul | solution.py:104
  104.0 19.9 %copy.13 = f32[512,27,256]{2,1,0:T(8,128)} copy(f32[512,27,256]{0,2,1:T(8,128)} %bitcast.181) | data formatting | bytes 28311552 | tf_op jit(solution)/shard_map/mul | solution.py:104
  123.9 150.5 %all-to-all-done = bf16[64,8,27,256]{3,1,2,0:T(8,128)(2,1)} async-done(((bf16[64,8,27,256]{3,1,2,0:T(8,128)(2,1)}), bf16[64,8,27,256]{3,1,2,0:T(8,128)(2,1)}, u32[]{:S(2)}, u32[]{:S(2)}) %all-to-all-start) | async-done | bytes 7077920 | tf_op jit(solution)/shard_map/all_to_all | solution.py:64
  274.4 3.9 copy.18
  288.4 96.4 %all-gather.2.cloned.1.call-done = bf16[512,27,256]{2,0,1:T(8,128)(2,1)} async-done(((bf16[8,27,256]{2,0,1:T(8,128)(2,1)}), bf16[512,27,256]{2,0,1:T(8,128)(2,1)}) %all-gather.2.cloned.1.call-update) | async-done | bytes 7077904 | tf_op jit(solution)/shard_map/all_gather | solution.py:73
  384.9 1.5 fusion.89
  386.3 1.7 convolution_add_fusion.25
  397.9 406.2 %reduce-scatter.2.cloned.1.call-done = f32[8,27,256]{2,1,0:T(8,128)} async-done(((f32[512,27,256]{2,1,0:T(8,128)}), f32[8,27,256]{2,1,0:T(8,128)}) %reduce-scatter.2.cloned.1.call-update) | async-done | bytes 221200 | tf_op jit(solution)/shard_map/reduce_scatter | solution.py:103
  806.0 51.3 %all-to-all-start.1 = ((bf16[4,8,27,256]{3,1,2,0:T(8,128)(2,1)}), bf16[4,8,27,256]{3,1,2,0:T(8,128)(2,1)}, u32[]{:S(2)}, u32[]{:S(2)}) async-start(bf16[4,8,27,256]{3,1,2,0:T(8,128)(2,1)} %broadcast_in_dim.15), calls=%async_computation.2 | async-start | bytes 884736 | tf_op jit(solution)/shard_map/all_to_all | solution.py:24
  857.3 2.3 fusion
  861.6 2.3 fusion.63
  863.9 4.4 all-to-all-done.1
  868.3 1.8 convert_reduce_fusion
  (86 shorter events, 45.4 us)
Async XLA Ops:
  7.2 377.7 %all-gather.2.cloned.1.call-start = ((), (), s32[]{:S(2)}) async-start(), calls=%async_computation.3 | async-start | bytes 7188480 | tf_op jit(solution)/shard_map/all_gather | solution.py:73
  7.9 14.6 %copy-start.2 = (bf16[8,27,256]{2,0,1:T(8,128)(2,1)S(1)}, bf16[8,27,256]{2,0,1:T(8,128)(2,1)}, u32[]{:S(2)}) copy-start(bf16[8,27,256]{2,0,1:T(8,128)(2,1)} %param.4) | copy-start | bytes 331780
  10.4 24.8 %collective-permute-start = (bf16[1,1,16,16,768]{4,3,2,1,0:T(8,128)(2,1)S(1)}, bf16[1,1,16,16,768]{4,3,2,1,0:T(8,128)(2,1)S(1)}, u32[]{:S(2)}, u32[]{:S(2)}) collective-permute-start(bf16[1,1,16,16,768]{4,3,2,1,0:T(8,128)(2,1)S(1)} %get-tuple-element.3), channel_id=1, source_target_pairs={{0,64},{64,128},{128,192},{1,65},{65,129},{129,193},{2,66},{66,130... | collective-permute-start | bytes 1179656 | tf_op jit(solution)/shard_map/ppermute | solution.py:14
  20.6 22.1 %collective-permute-start.1 = (bf16[1,1,16,16,768]{4,3,2,1,0:T(8,128)(2,1)S(1)}, bf16[1,1,16,16,768]{4,3,2,1,0:T(8,128)(2,1)S(1)}, u32[]{:S(2)}, u32[]{:S(2)}) collective-permute-start(bf16[1,1,16,16,768]{4,3,2,1,0:T(8,128)(2,1)S(1)} %get-tuple-element.4), channel_id=1, source_target_pairs={{64,0},{128,64},{192,128},{65,1},{129,65},{193,129},{66,2},{130,66... | collective-permute-start | bytes 1179656 | tf_op jit(solution)/shard_map/ppermute | solution.py:17
  25.9 248.6 %all-to-all-start = ((bf16[64,8,27,256]{3,1,2,0:T(8,128)(2,1)}), bf16[64,8,27,256]{3,1,2,0:T(8,128)(2,1)}, u32[]{:S(2)}, u32[]{:S(2)}) async-start(bf16[64,8,27,256]{3,1,2,0:T(8,128)(2,1)} %stack.2), calls=%async_computation | async-start | bytes 14155776 | tf_op jit(solution)/shard_map/all_to_all | solution.py:64
  35.1 769.0 %reduce-scatter.2.cloned.1.call-start = ((), (), s32[]{:S(2)}) async-start(), calls=%async_computation.4 | async-start | bytes 17039360 | tf_op jit(solution)/shard_map/reduce_scatter | solution.py:103
  278.3 8.9 %copy-start = (bf16[64,8,27,256]{3,1,0,2:T(8,128)(2,1)}, bf16[64,8,27,256]{3,1,0,2:T(8,128)(2,1)S(1)}, u32[]{:S(2)}) copy-start(bf16[64,8,27,256]{3,1,0,2:T(8,128)(2,1)S(1)} %copy.18) | copy-start | bytes 21233668
  384.9 3.2 copy-start.1
  806.0 62.3 %all-to-all-start.1 = ((bf16[4,8,27,256]{3,1,2,0:T(8,128)(2,1)}), bf16[4,8,27,256]{3,1,2,0:T(8,128)(2,1)}, u32[]{:S(2)}, u32[]{:S(2)}) async-start(bf16[4,8,27,256]{3,1,2,0:T(8,128)(2,1)} %broadcast_in_dim.15), calls=%async_computation.2 | async-start | bytes 884736 | tf_op jit(solution)/shard_map/all_to_all | solution.py:24
Sparse Core Ops, SparseCore 0:
  9.7 375.1 all-gather.1
  387.4 416.7 reduce-scatter.1
